TPU v7x, 32 devices: a whole 2x2x4 slice. The times are simulated.
32 devices in a mesh: tp: 4 (over z), dp: 8 (over y, x, core).
Axes of the slice: x: 2, y: 2, z: 4, core: 2. Of those that a mesh axis runs over, the one named last changes fastest.
Arguments:
- w_query: bfloat16 [16, 1024, 1024], P(None, ('dp', 'tp'))
- w_key: bfloat16 [16, 1024, 1024], P(None, ('dp', 'tp'))
- w_value: bfloat16 [16, 1024, 1024], P(None, ('dp', 'tp'))
- w_out: bfloat16 [16, 1024, 1024], P(None, ('dp', 'tp'))
- w_gate: bfloat16 [16, 1024, 2816], P(None, ('dp', 'tp'))
- w_up: bfloat16 [16, 1024, 2816], P(None, ('dp', 'tp'))
- w_down: bfloat16 [16, 2816, 1024], P(None, ('dp', 'tp'))
- w_head: bfloat16 [1024, 151936], P(('dp', 'tp'))
Outputs:
- output 1: bfloat16 [16, 3072, 1024], P(None, 'tp')
- output 2: bfloat16 [16, 1024, 1024], P(None, None, 'tp')
- output 3: bfloat16 [16, 5632, 1024], P(None, 'tp')
- output 4: bfloat16 [16, 1024, 2816], P(None, None, 'tp')
- output 5: bfloat16 [151936, 1024], P('tp')
All inputs are finite; a program needn't handle non-finite values.
Results may differ from a plain program's by a relative error of at most 0.001.
Values are sent between devices in bfloat16 or wider.
A program may use at most 1 GiB of HBM per device.

v0:
```python
import jax
import jax.numpy as jnp
from jax import lax
from jax.sharding import PartitionSpec as P


def to_columns(local):
    row_axis = local.ndim - 2
    swapped = lax.all_to_all(local, "tp", split_axis=local.ndim - 1, concat_axis=row_axis, tiled=True)
    gathered = lax.all_gather(swapped, "dp", axis=row_axis, tiled=True)
    return jnp.swapaxes(gathered, row_axis, row_axis + 1)


def to_rows(local, tp_size, dp_size):
    layers, block_rows, columns = local.shape
    gathered = lax.all_gather(local, "dp", axis=1, tiled=False)
    grouped = gathered.reshape(layers, tp_size, dp_size // tp_size, 1, block_rows, columns)
    swapped = lax.all_to_all(grouped, "tp", split_axis=1, concat_axis=3, tiled=True)
    return jnp.swapaxes(swapped.reshape(layers, dp_size * block_rows, columns), 1, 2)


def solution(mesh):
    tp_size = mesh.shape["tp"]
    dp_size = mesh.shape["dp"]
    train_stack = P(None, ("dp", "tp"), None)
    train_head = P(("dp", "tp"), None)
    fused_stack = P(None, "tp", None)
    last_stack = P(None, None, "tp")
    head_rows = P("tp", None)

    def local_sync(w_query, w_key, w_value, w_out, w_gate, w_up, w_down, w_head):
        qkv_block = jnp.concatenate([to_columns(w_query), to_columns(w_key), to_columns(w_value)], axis=1)
        gate_up_block = jnp.concatenate([to_columns(w_gate), to_columns(w_up)], axis=1)
        return (
            qkv_block,
            to_rows(w_out, tp_size, dp_size),
            gate_up_block,
            to_rows(w_down, tp_size, dp_size),
            to_columns(w_head),
        )

    return jax.shard_map(
        local_sync,
        mesh=mesh,
        in_specs=(train_stack,) * 7 + (train_head,),
        out_specs=(fused_stack, last_stack, fused_stack, last_stack, head_rows),
        check_vma=False,
    )
```

profile of v0, /device:TPU:0, one launch (start us, length us, event | category | flops | bytes accessed | tf_op | source)
XLA Modules:
  0.0 1456.3 jit_solution(16232678800100403072)
XLA Ops:
  20.2 31.9 %all_to_all.139 = bf16[4,2,65536]{2,1,0:T(2,128)(2,1)S(1)} all-to-all(bf16[4,2,65536]{2,1,0:T(2,128)(2,1)S(1)} %reshape.35), channel_id=1, replica_groups=mesh['tp'=4,'dp'=8] {'tp'}, dimensions={0} | all-to-all | bytes 2097152 | tf_op jit(solution)/shard_map/all_to_all | solution.py:9
  72.2 28.3 %all_to_all.140 = bf16[4,2,65536]{2,1,0:T(2,128)(2,1)S(1)} all-to-all(bf16[4,2,65536]{2,1,0:T(2,128)(2,1)S(1)} %reshape.39), channel_id=1, replica_groups=mesh['tp'=4,'dp'=8] {'tp'}, dimensions={0} | all-to-all | bytes 2097152 | tf_op jit(solution)/shard_map/all_to_all | solution.py:9
  120.6 28.0 %all_to_all.141 = bf16[4,2,65536]{2,1,0:T(2,128)(2,1)S(1)} all-to-all(bf16[4,2,65536]{2,1,0:T(2,128)(2,1)S(1)} %reshape.37), channel_id=1, replica_groups=mesh['tp'=4,'dp'=8] {'tp'}, dimensions={0} | all-to-all | bytes 2097152 | tf_op jit(solution)/shard_map/all_to_all | solution.py:9
  158.5 13.0 copy.72
  171.6 13.0 reshape.43
  184.6 67.3 %all_to_all.142 = bf16[4,2,180224]{2,1,0:T(2,128)(2,1)} all-to-all(bf16[4,2,180224]{2,1,0:T(2,128)(2,1)S(1)} %reshape.43), channel_id=1, replica_groups=mesh['tp'=4,'dp'=8] {'tp'}, dimensions={0} | all-to-all | bytes 5767168 | tf_op jit(solution)/shard_map/all_to_all | solution.py:9
  251.8 8.9 reshape.44
  260.7 13.4 copy.73
  274.2 11.2 copy.74
  285.4 13.0 reshape.41
  298.4 68.0 %all_to_all.143 = bf16[4,2,180224]{2,1,0:T(2,128)(2,1)} all-to-all(bf16[4,2,180224]{2,1,0:T(2,128)(2,1)S(1)} %reshape.41), channel_id=1, replica_groups=mesh['tp'=4,'dp'=8] {'tp'}, dimensions={0} | all-to-all | bytes 5767168 | tf_op jit(solution)/shard_map/all_to_all | solution.py:9
  375.3 13.2 copy.75
  388.7 11.2 all_to_all.127
  408.4 219.2 %all_to_all.144 = bf16[32,4,37984]{2,0,1:T(8,128)(2,1)} all-to-all(bf16[32,4,37984]{2,0,1:T(8,128)(2,1)} %copy.78), channel_id=1, replica_groups=mesh['tp'=4,'dp'=8] {'tp'}, dimensions={1} | all-to-all | bytes 19447808 | tf_op jit(solution)/shard_map/all_to_all | solution.py:9
  642.0 20.7 %copy.76 = bf16[16,4,2,1,88,1024]{5,4,2,0,3,1:T(8,128)(2,1)} copy(bf16[16,4,2,1,88,1024]{5,4,2,1,0,3:T(8,128)(2,1)} %bitcast.60) | data formatting | bytes 46137344 | tf_op jit(solution)/shard_map/reshape | solution.py:17
  662.7 161.4 %all-to-all-done.3 = bf16[16,4,2,1,32,1024]{5,4,2,0,3,1:T(8,128)(2,1)} async-done(((bf16[16,4,2,1,32,1024]{5,4,2,0,3,1:T(8,128)(2,1)}), bf16[16,4,2,1,32,1024]{5,4,2,0,3,1:T(8,128)(2,1)}, u32[]{:S(2)}, u32[]{:S(2)}) %all-to-all-start.3) | async-done | bytes 8388640 | tf_op jit(solution)/shard_map/all_to_all | solution.py:18
  832.2 20.2 %pad_maximum_fusion.1 = bf16[16,768,1024]{1,2,0:T(8,128)(2,1)} fusion(bf16[16,256,1024]{1,2,0:T(8,128)(2,1)} %bitcast.71, bf16[16,256,1024]{1,2,0:T(8,128)(2,1)} %bitcast.73, bf16[16,256,1024]{1,2,0:T(8,128)(2,1)} %bitcast.72), kind=kLoop, calls=%fused_computation.1 | loop fusion | flops 75497472 | bytes 50331648 | tf_op jit(solution)/shard_map/concatenate | solution.py:32
  852.4 32.6 %copy.79 = bf16[16,768,1024]{2,1,0:T(8,128)(2,1)} copy(bf16[16,768,1024]{1,2,0:T(8,128)(2,1)} %pad_maximum_fusion.1) | data formatting | bytes 50331648
  893.7 12.2 copy.80
  905.9 32.3 %pad_maximum_fusion = bf16[16,1408,1024]{1,2,0:T(8,128)(2,1)} fusion(bf16[16,704,1024]{1,2,0:T(8,128)(2,1)} %bitcast.59, bf16[16,704,1024]{1,2,0:T(8,128)(2,1)} %bitcast.58), kind=kLoop, calls=%fused_computation | loop fusion | flops 92274688 | bytes 92274688 | tf_op jit(solution)/shard_map/concatenate | solution.py:33
  938.2 56.1 %copy.81 = bf16[16,1408,1024]{2,1,0:T(8,128)(2,1)} copy(bf16[16,1408,1024]{1,2,0:T(8,128)(2,1)} %pad_maximum_fusion) | data formatting | bytes 92274688
  994.3 334.8 %all-to-all-done.6 = bf16[16,4,2,1,88,1024]{5,4,2,0,3,1:T(8,128)(2,1)} async-done(((bf16[16,4,2,1,88,1024]{5,4,2,0,3,1:T(8,128)(2,1)}), bf16[16,4,2,1,88,1024]{5,4,2,0,3,1:T(8,128)(2,1)}, u32[]{:S(2)}, u32[]{:S(2)}) %all-to-all-start.6) | async-done | bytes 23068704 | tf_op jit(solution)/shard_map/all_to_all | solution.py:18
  1329.0 20.3 %copy.77 = bf16[16,4,2,1,88,1024]{5,4,1,2,0,3:T(8,128)(2,1)} copy(bf16[16,4,2,1,88,1024]{5,4,2,0,3,1:T(8,128)(2,1)} %all-to-all-done.6) | data formatting | bytes 46137344 | tf_op jit(solution)/shard_map/all_to_all | solution.py:18
  1349.4 100.1 %copy.82 = bf16[37984,1024]{1,0:T(8,128)(2,1)} copy(bf16[37984,1024]{0,1:T(8,128)(2,1)} %bitcast.32) | data formatting | bytes 155582464
  (51 shorter events, 111.9 us)
Async XLA Ops:
  7.2 620.5 %all-gather.23.cloned.1.call-start = ((), (), s32[]{:S(2)}) async-start(), calls=%async_computation.14 | async-start | bytes 9437184 | tf_op jit(solution)/shard_map/all_gather | solution.py:16
  7.9 634.1 %all-gather.25.cloned.1.call-start = ((), (), s32[]{:S(2)}) async-start(), calls=%async_computation.15 | async-start | bytes 25952256 | tf_op jit(solution)/shard_map/all_gather | solution.py:16
  8.6 823.5 %all-gather.15.cloned.1.call-start = ((), (), s32[]{:S(2)}) async-start(), calls=%async_computation.10 | async-start | bytes 9437184 | tf_op jit(solution)/shard_map/all_gather | solution.py:10
  14.5 47.3 %copy-start.1 = (bf16[16,32,1024]{2,1,0:T(8,128)(2,1)S(1)}, bf16[16,32,1024]{2,1,0:T(8,128)(2,1)}, u32[]{:S(2)}) copy-start(bf16[16,32,1024]{2,1,0:T(8,128)(2,1)} %param.8) | copy-start | bytes 3145732
  61.8 770.4 %all-gather.11.cloned.1.call-start = ((), (), s32[]{:S(2)}) async-start(), calls=%async_computation.8 | async-start | bytes 9437184 | tf_op jit(solution)/shard_map/all_gather | solution.py:10
  66.6 43.8 %copy-start.2 = (bf16[16,32,1024]{2,1,0:T(8,128)(2,1)S(1)}, bf16[16,32,1024]{2,1,0:T(8,128)(2,1)}, u32[]{:S(2)}) copy-start(bf16[16,32,1024]{2,1,0:T(8,128)(2,1)} %param.9) | copy-start | bytes 3145732
  110.3 722.0 %all-gather.13.cloned.1.call-start = ((), (), s32[]{:S(2)}) async-start(), calls=%async_computation.9 | async-start | bytes 9437184 | tf_op jit(solution)/shard_map/all_gather | solution.py:10
  158.3 747.6 %all-gather.17.cloned.1.call-start = ((), (), s32[]{:S(2)}) async-start(), calls=%async_computation.11 | async-start | bytes 28311552 | tf_op jit(solution)/shard_map/all_gather | solution.py:10
  260.7 13.5 copy-start
  274.1 631.8 %all-gather.19.cloned.1.call-start = ((), (), s32[]{:S(2)}) async-start(), calls=%async_computation.12 | async-start | bytes 28311552 | tf_op jit(solution)/shard_map/all_gather | solution.py:10
  388.5 960.9 %all-gather.21.cloned.1.call-start = ((), (), s32[]{:S(2)}) async-start(), calls=%async_computation.13 | async-start | bytes 87588864 | tf_op jit(solution)/shard_map/all_gather | solution.py:10
  636.3 187.8 %all-to-all-start.3 = ((bf16[16,4,2,1,32,1024]{5,4,2,0,3,1:T(8,128)(2,1)}), bf16[16,4,2,1,32,1024]{5,4,2,0,3,1:T(8,128)(2,1)}, u32[]{:S(2)}, u32[]{:S(2)}) async-start(bf16[16,4,2,1,32,1024]{5,4,2,0,3,1:T(8,128)(2,1)} %copy.70), calls=%async_computation.3 | async-start | bytes 16777216 | tf_op jit(solution)/shard_map/all_to_all | solution.py:18
  824.1 504.9 %all-to-all-start.6 = ((bf16[16,4,2,1,88,1024]{5,4,2,0,3,1:T(8,128)(2,1)}), bf16[16,4,2,1,88,1024]{5,4,2,0,3,1:T(8,128)(2,1)}, u32[]{:S(2)}, u32[]{:S(2)}) async-start(bf16[16,4,2,1,88,1024]{5,4,2,0,3,1:T(8,128)(2,1)} %copy.76), calls=%async_computation.6 | async-start | bytes 46137344 | tf_op jit(solution)/shard_map/all_to_all | solution.py:18
Sparse Core Ops, SparseCore 0:
  9.9 56.6 all-gather.22
  68.5 116.3 all-gather.24
  187.3 53.8 all-gather.14
  243.0 53.8 all-gather.10
  298.7 53.8 all-gather.12
  354.3 125.1 all-gather.16
  482.0 125.1 all-gather.18
  627.8 348.1 all-gather.20
where the time goes:
time: 1460 us
  waiting for transfers between devices  498 us (34%)
  blocking collectives  443 us (30%)
  local copies, waits for them, and re-layouts  435 us (30%)
  other arithmetic  52.5 us (4%)
    all_to_all x2, waiting for transfers between devices, to_rows(): lax.all_to_all(grouped, 'tp', split_axis=1, concat_axis=3, tiled=True)  496 us
    all_to_all x6, blocking collectives, to_columns(): lax.all_to_all(local, 'tp', split_axis=local.ndim - 1, concat_axis=row_ax...  443 us
    unnamed x25, local copies, waits for them, and re-layouts  312 us
    all_to_all x10, local copies, waits for them, and re-layouts, to_columns(): lax.all_to_all(local, 'tp', split_axis=local.ndim - 1, concat_axis=row_ax...  64.9 us
    concatenate x1, other arithmetic, local_sync(): jnp.concatenate([to_columns(w_gate), to_columns(w_up)], axis=1)  32.3 us
    reshape x2, local copies, waits for them, and re-layouts, to_rows(): gathered.reshape(layers, tp_size, dp_size // tp_size, 1, block_rows, colu...  29.3 us
  transfers between devices with their start and end apart: 10, of which 2 were waited for; matrix products, arithmetic and copies ran while one was open for 26% of the time, Pallas kernels for 0%

commit v1 on v0

v1 whole, which is shorter than its diff:
```python
import functools

import jax
import jax.numpy as jnp
from jax import lax
from jax.experimental import pallas as pl
from jax.experimental.pallas import tpu as pltpu
from jax.sharding import PartitionSpec as P

MESH = pl.DeviceIdType.MESH
LANES = 128
AHEAD = 4
LAG = 2
SCRATCH_TILES = 3


class Plan:
    def __init__(self, tp, dp, w_query, w_gate, w_out, w_down, w_head):
        self.tp, self.dp = tp, dp
        self.layers, self.rows, columns = w_query.shape
        self.part = columns // tp
        self.wide = w_gate.shape[2] // tp
        self.vocab = w_head.shape[1] // tp
        self.head_tiles = w_head.shape[1] // LANES
        self.chunk = 3 * self.part + 2 * self.wide
        self.wide_window = -(-self.wide // LANES) * LANES
        self.layer_window = 3 * self.part + 2 * self.wide_window
        self.head_chunks = -(-self.vocab // self.chunk)
        self.tail = self.vocab - (self.head_chunks - 1) * self.chunk
        self.chunks = self.layers + self.head_chunks
        self.tail_window = -(-(self.tail + LANES) // LANES) * LANES
        self.window_tiles = (self.head_chunks - 1) * self.chunk // LANES + self.tail_window // LANES
        self.out_rows, self.down_rows = w_out.shape[1], w_down.shape[1]
        self.share = self.layers // dp

    def wide_base(self, rank):
        return (self.wide * rank) // LANES

    def head_base(self, rank):
        base = (self.vocab * rank) // LANES
        return base - (rank // (self.tp - 1)) * (self.vocab * (self.tp - 1) // LANES + self.window_tiles - self.head_tiles)


def gather_kernel(plan, q, k, v, o, g, u, d, h, slabs, outs, downs, zbuf, tbuf, z_recv, z_send, local, x_recv, y_recv,
                  a_recv, b_recv, pair_recv, send, share_recv, share_send):
    z, dp = lax.axis_index("tp"), lax.axis_index("dp")
    core, x, y = dp % 2, (dp // 2) % 2, dp // 4
    x_peer = y * 4 + (1 - x) * 2 + core
    y_peer = (1 - y) * 4 + x * 2 + core
    diagonal = (1 - y) * 4 + (1 - x) * 2 + core
    pair = dp + 1 - 2 * core
    rows, chunk, tail = plan.rows, plan.chunk, plan.tail
    layers, last = plan.layers, plan.chunks - 1
    my_rows = pl.ds(pl.multiple_of(z * rows, rows), rows)

    def lanes(first_tile, width):
        return pl.ds(pl.multiple_of(first_tile * LANES, LANES), width)

    def exchange(pieces, index):
        for step in range(1, plan.tp):
            rank = (z + step) % plan.tp
            for source, column, width in pieces(rank):
                pltpu.make_async_remote_copy(
                    source, zbuf.at[index, my_rows, pl.ds(column, width)], z_send.at[index], z_recv.at[index],
                    device_id={"tp": rank}, device_id_type=MESH,
                ).start()
        for source, column, width in pieces(z):
            pltpu.make_async_copy(source, zbuf.at[index, my_rows, pl.ds(column, width)], z_recv.at[index]).start()

    def layer_pieces(layer):
        def pieces(rank):
            part, wide = plan.part, plan.wide_window
            narrow = lanes(rank * (part // LANES), part)
            window = lanes(plan.wide_base(rank), wide)
            return [
                (q.at[layer, :, narrow], 0, part),
                (k.at[layer, :, narrow], part, part),
                (v.at[layer, :, narrow], 2 * part, part),
                (g.at[layer, :, window], 3 * part, wide),
                (u.at[layer, :, window], 3 * part + wide, wide),
            ]
        return pieces

    def head_pieces(step, width):
        def pieces(rank):
            return [(h.at[:, lanes(plan.head_base(rank) + step * (chunk // LANES), width)], 0, width)]
        return pieces

    def start_exchange(index):
        @pl.when(index < layers)
        def _():
            exchange(layer_pieces(index), index)

        @pl.when((index >= layers) & (index < last))
        def _():
            exchange(head_pieces(index - layers, chunk), index)

        @pl.when(index == last)
        def _():
            exchange(head_pieces(last - layers, plan.tail_window), last)

    def wait_for(ref, sem):
        pltpu.make_async_copy(ref, ref, sem).wait()

    def wait_exchange(index, width):
        wait_for(zbuf.at[index, :, pl.ds(0, width)], z_recv.at[index])

    def turn(slot, tile, index, source_tile):
        tbuf[slot, pl.ds(tile * LANES, LANES), :] = zbuf[index, :, pl.ds(source_tile * LANES, LANES)].T

    def store(slot, first, index, to, count):
        return pltpu.make_async_copy(
            tbuf.at[slot, pl.ds(first, count), :], slabs.at[dp, index, pl.ds(to, count), :], local.at[slot]
        )

    def make_layer(index, slot):
        wait_exchange(index, plan.layer_window)
        for tile in range(plan.layer_window // LANES):
            turn(slot, tile, index, tile)
        shift = plan.wide * z - plan.wide_base(z) * LANES
        narrow, wide, window = 3 * plan.part, plan.wide, plan.wide_window
        store(slot, 0, index, 0, narrow).start()
        store(slot, pl.multiple_of(narrow + shift, 16), index, narrow, wide).start()
        store(slot, pl.multiple_of(narrow + window + shift, 16), index, narrow + wide, wide).start()

    head_shift = plan.vocab * z - plan.head_base(z) * LANES

    def make_head(index, slot):
        @pl.when(index == layers)
        def _():
            wait_exchange(index, chunk)

        @pl.when(index < last - 1)
        def _():
            wait_exchange(index + 1, chunk)

        @pl.when(index == last - 1)
        def _():
            wait_exchange(last, plan.tail_window)

        tiles = chunk // LANES
        for tile in range(tiles):
            turn(slot, tile, index, tile)
        for tile in range(2):
            turn(slot, tiles + tile, index + 1, tile)
        store(slot, pl.multiple_of(head_shift, 16), index, 0, chunk).start()

    def make_tail(slot):
        for tile in range(plan.tail_window // LANES):
            turn(slot, tile, last, tile)
        store(slot, pl.multiple_of(head_shift, 16), last, 0, tail).start()

    def push(owner, index, first, count, recv, to):
        part = slabs.at[owner, index, pl.ds(first, count), :]
        pltpu.make_async_remote_copy(
            part, part, send.at[index], recv.at[index], device_id={"dp": to}, device_id_type=MESH
        ).start()

    def wait_slab(owner, index, first, count, sem):
        wait_for(slabs.at[owner, index, pl.ds(first, count), :], sem.at[index])

    def send_own(index, slot, count):
        wait_for(slabs.at[dp, index, pl.ds(0, count), :], local.at[slot])
        push(dp, index, 0, count, x_recv, x_peer)
        push(dp, index, 0, count, y_recv, y_peer)
        push(dp, index, 0, count, pair_recv, pair)

    def forward(index, count):
        half = count // 2
        wait_slab(x_peer, index, 0, count, x_recv)
        push(x_peer, index, half, half, b_recv, y_peer)
        push(x_peer, index, 0, count, pair_recv, pair)
        wait_slab(y_peer, index, 0, count, y_recv)
        push(y_peer, index, 0, half, a_recv, x_peer)
        push(y_peer, index, 0, count, pair_recv, pair)

    def forward_diagonal(index, count):
        half = count // 2
        wait_slab(diagonal, index, 0, half, a_recv)
        wait_slab(diagonal, index, half, half, b_recv)
        push(diagonal, index, 0, count, pair_recv, pair)

    def finish(index, count, window):
        wait_for(slabs.at[pl.ds(0, 7), index, pl.ds(0, count), :], send.at[index])
        wait_for(slabs.at[pl.ds(0, 4), index, pl.ds(0, count), :], pair_recv.at[index])
        wait_for(zbuf.at[index, pl.ds(0, (plan.tp - 1) * rows), pl.ds(0, window)], z_send.at[index])

    for index in range(AHEAD):
        start_exchange(index)

    rank = dp // 2
    place = (dp % 2) * plan.tp + z
    stays = rank == z
    shares = ((d, downs, plan.down_rows), (o, outs, plan.out_rows))
    for step in range(plan.dp):
        to = (dp + step) % plan.dp
        for n, (source, target, count) in enumerate(shares):
            piece = source.at[pl.ds(to * plan.share, plan.share), :, :]
            landing = target.at[:, pl.ds(pl.multiple_of(place * count, 8), count), :]

            def start_remote(piece=piece, landing=landing, n=n, to=to):
                pltpu.make_async_remote_copy(
                    piece, landing, share_send.at[n], share_recv.at[n],
                    device_id={"dp": to, "tp": rank}, device_id_type=MESH,
                ).start()

            if step:
                start_remote()
            else:
                pl.when(jnp.logical_not(stays))(start_remote)

                @pl.when(stays)
                def _(piece=piece, landing=landing, n=n):
                    pltpu.make_async_copy(piece, landing, share_recv.at[n]).start()

    def step(index, _):
        slot = index % 2

        @pl.when(index + AHEAD < plan.chunks)
        def _():
            start_exchange(index + AHEAD)

        @pl.when(index < layers)
        def _():
            make_layer(index, slot)

        @pl.when(index >= layers)
        def _():
            make_head(index, slot)

        send_own(index, slot, chunk)

        @pl.when(index >= LAG)
        def _():
            forward(index - LAG, chunk)

        @pl.when(index >= 2 * LAG)
        def _():
            forward_diagonal(index - 2 * LAG, chunk)

        return 0

    lax.fori_loop(0, last, step, 0)
    make_tail(last % 2)
    send_own(last, last % 2, tail)
    for index in range(last - LAG, last):
        forward(index, chunk)
    forward(last, tail)
    for index in range(last - 2 * LAG, last):
        forward_diagonal(index, chunk)
    forward_diagonal(last, tail)

    def drain(index, _):
        @pl.when(index < layers)
        def _():
            finish(index, chunk, plan.layer_window)

        @pl.when(index >= layers)
        def _():
            finish(index, chunk, chunk)

        return 0

    lax.fori_loop(0, last, drain, 0)
    finish(last, tail, plan.tail_window)
    for n, (_, target, count) in enumerate(shares):
        wait_for(target, share_recv.at[n])
        wait_for(target.at[:, pl.ds(0, (plan.dp - 1) * count), :], share_send.at[n])

        @pl.when(jnp.logical_not(stays))
        def _(target=target, count=count, n=n):
            wait_for(target.at[:, pl.ds(0, count), :], share_send.at[n])


def gather(plan, *args):
    dma = pltpu.SemaphoreType.DMA
    per_chunk = dma((plan.chunks,))
    columns = args[3].shape[2]
    hbm = pl.BlockSpec(memory_space=pltpu.HBM)
    return pl.pallas_call(
        functools.partial(gather_kernel, plan),
        out_shape=(
            jax.ShapeDtypeStruct((plan.dp, plan.chunks, plan.chunk, LANES), jnp.bfloat16),
            jax.ShapeDtypeStruct((plan.share, 8 * plan.out_rows, columns), jnp.bfloat16),
            jax.ShapeDtypeStruct((plan.share, 8 * plan.down_rows, columns), jnp.bfloat16),
        ),
        in_specs=[hbm] * 8,
        out_specs=(hbm,) * 3,
        scratch_shapes=[
            pltpu.VMEM((plan.chunks, plan.tp * plan.rows, plan.layer_window), jnp.bfloat16),
            pltpu.VMEM((2, plan.chunk + 2 * LANES, LANES), jnp.bfloat16),
            per_chunk, per_chunk, dma((2,)),
            per_chunk, per_chunk, per_chunk, per_chunk, per_chunk, per_chunk,
            dma((2,)), dma((2,)),
        ],
        compiler_params=pltpu.CompilerParams(has_side_effects=True),
        name="gather",
    )(*args)


def place_layers(plan, slabs):
    narrow, wide = 3 * plan.part, 2 * plan.wide

    def body(slab, qkv, gate_up):
        for i in range(plan.dp):
            lanes = pl.ds(i * LANES, LANES)
            qkv[0, :, lanes] = slab[i, 0, :narrow, :]
            gate_up[0, :, lanes] = slab[i, 0, narrow:, :]

    width = plan.dp * LANES
    bytes_moved = 4 * plan.layers * plan.chunk * width
    return pl.pallas_call(
        body,
        grid=(plan.layers,),
        in_specs=[pl.BlockSpec((plan.dp, 1, plan.chunk, LANES), lambda i: (0, i, 0, 0))],
        out_specs=(
            pl.BlockSpec((1, narrow, width), lambda i: (i, 0, 0)),
            pl.BlockSpec((1, wide, width), lambda i: (i, 0, 0)),
        ),
        out_shape=(
            jax.ShapeDtypeStruct((plan.layers, narrow, width), jnp.bfloat16),
            jax.ShapeDtypeStruct((plan.layers, wide, width), jnp.bfloat16),
        ),
        cost_estimate=pl.CostEstimate(flops=10**10, bytes_accessed=bytes_moved, transcendentals=0),
        name="place_layers",
    )(slabs)


def place_head(plan, slabs):
    def body(slab, head):
        for i in range(plan.dp):
            head[:, pl.ds(i * LANES, LANES)] = slab[i, 0]

    width = plan.dp * LANES
    return pl.pallas_call(
        body,
        grid=(plan.head_chunks,),
        in_specs=[pl.BlockSpec((plan.dp, 1, plan.chunk, LANES), lambda i: (0, plan.layers + i, 0, 0))],
        out_specs=pl.BlockSpec((plan.chunk, width), lambda i: (i, 0)),
        out_shape=jax.ShapeDtypeStruct((plan.vocab, width), jnp.bfloat16),
        cost_estimate=pl.CostEstimate(flops=10**10, bytes_accessed=4 * plan.vocab * width, transcendentals=0),
        name="place_head",
    )(slabs)


def solution(mesh):
    train_stack = P(None, ("dp", "tp"), None)
    train_head = P(("dp", "tp"), None)
    fused_stack = P(None, "tp", None)
    last_stack = P(None, None, "tp")
    head_rows = P("tp", None)

    def local_sync(w_query, w_key, w_value, w_out, w_gate, w_up, w_down, w_head):
        plan = Plan(mesh.shape["tp"], mesh.shape["dp"], w_query, w_gate, w_out, w_down, w_head)
        slabs, outs, downs = gather(plan, w_query, w_key, w_value, w_out, w_gate, w_up, w_down, w_head)
        o_block = lax.all_gather(outs, "dp", axis=0, tiled=True)
        down_block = lax.all_gather(downs, "dp", axis=0, tiled=True)
        qkv_block, gate_up_block = place_layers(plan, slabs)
        head_block = place_head(plan, slabs)
        return (
            qkv_block,
            jnp.swapaxes(o_block, 1, 2),
            gate_up_block,
            jnp.swapaxes(down_block, 1, 2),
            head_block,
        )

    return jax.shard_map(
        local_sync,
        mesh=mesh,
        in_specs=(train_stack,) * 7 + (train_head,),
        out_specs=(fused_stack, last_stack, fused_stack, last_stack, head_rows),
        check_vma=False,
    )
```

time: 1460 us -> 1120 us (0.77)
  Pallas kernels: 0 us -> 1020 us
  waiting for transfers between devices: 498 us -> 49.3 us
  blocking collectives: 443 us -> 0 us
  local copies, waits for them, and re-layouts: 435 us -> 32.5 us
  other arithmetic: 52.5 us -> 0 us
    pallas_call x0 -> x3, Pallas kernels: none -> 1020 us  [the longest x1 906 us: gather(): pl.pallas_call(functools.partial(gather_kernel, plan), out_shape=(jax.Sha...]
    all_to_all x2 -> x0, waiting for transfers between devices: 496 us -> none  [to_rows(): lax.all_to_all(grouped, 'tp', split_axis=1, concat_axis=3, tiled=True)]
    all_to_all x6 -> x0, blocking collectives: 443 us -> none  [to_columns(): lax.all_to_all(local, 'tp', split_axis=local.ndim - 1, concat_axis=row_ax...]
    unnamed x25 -> x2, local copies, waits for them, and re-layouts: 312 us -> 32.5 us
    all_to_all x12 -> x0, local copies, waits for them, and re-layouts: 93.9 us -> none  [the longest x10 64.9 us: to_columns(): lax.all_to_all(local, 'tp', split_axis=local.ndim - 1, concat_axis=row_ax...]
    concatenate x2 -> x0, other arithmetic: 52.5 us -> none  [the longest x1 32.3 us: local_sync(): jnp.concatenate([to_columns(w_gate), to_columns(w_up)], axis=1)]
    all_gather x8 -> x2, waiting for transfers between devices: 0.1 us -> 48.6 us  [the longest x1 48.6 us: local_sync(): down_block = lax.all_gather(downs, 'dp', axis=0, tiled=True)]
    reshape x2 -> x0, local copies, waits for them, and re-layouts: 29.3 us -> none  [to_rows(): gathered.reshape(layers, tp_size, dp_size // tp_size, 1, block_rows, colu...]
  transfers between devices with their start and end apart: 10 -> 2, of which waited for: 2 -> 1; matrix products, arithmetic and copies ran while one was open for 26% -> 1% of each run, Pallas kernels for 0% -> 10%
where the time goes in v1:
time: 1120 us; the launch traced here: 1110 us
  Pallas kernels  1020 us (91%)
  waiting for transfers between devices  49.3 us (4%)
  local copies, waits for them, and re-layouts  32.5 us (3%)
  between operations  14 us (1%)
    pallas_call x1, Pallas kernels, gather(): pl.pallas_call(functools.partial(gather_kernel, plan), out_shape=(jax.Sha...  906 us
    pallas_call x1, Pallas kernels, place_head(): pl.pallas_call(body, grid=(plan.head_chunks,), in_specs=[pl.BlockSpec((pl...  59.5 us
    pallas_call x1, Pallas kernels, place_layers(): pl.pallas_call(body, grid=(plan.layers,), in_specs=[pl.BlockSpec((plan.dp...  53.4 us
    all_gather x1, waiting for transfers between devices, local_sync(): down_block = lax.all_gather(downs, 'dp', axis=0, tiled=True)  48.6 us
    unnamed x2, local copies, waits for them, and re-layouts  32.5 us
  transfers between devices with their start and end apart: 2, of which 1 were waited for; matrix products, arithmetic and copies ran while one was open for 1% of the time, Pallas kernels for 10%

profile of v1, /device:TPU:0, one launch (start us, length us, event | category | flops | bytes accessed | tf_op | source)
XLA Modules:
  0.0 1114.4 jit_solution(15236191635990289869)
XLA Ops:
  7.2 0.0 all-gather.3.cloned.1.call-start
  7.2 905.5 %gather.1 = (bf16[8,34,2176,128]{3,2,1,0:T(8,128)(2,1)}, bf16[2,256,1024]{2,1,0:T(8,128)(2,1)}, bf16[2,704,1024]{2,1,0:T(8,128)(2,1)}) custom-call(bf16[16,32,1024]{2,1,0:T(8,128)(2,1)} %q.1, bf16[16,32,1024]{2,1,0:T(8,128)(2,1)} %k.1, bf16[16,32,1024]{2,1,0:T(8,128)(2,1)} %v.1, bf16[16,32,1024]{2,1,0:T(8,128)(2,1)} %o.1, bf16[16,32,2816]{2,1,0:T(8,128)(2,1)} %g.1, ...), custom_call_target="tpu_custom_call" | custom-call | tf_op jit(solution)/shard_map/gather/pallas_call | solution.py:280
  912.7 0.0 all-gather.3.cloned.1.call-update
  912.8 0.0 all-gather.5.cloned.1.call-start
  912.8 0.7 all-gather.5.cloned.1.call-update
  913.5 53.4 %place_layers.1 = (bf16[16,768,1024]{2,1,0:T(8,128)(2,1)}, bf16[16,1408,1024]{2,1,0:T(8,128)(2,1)}) custom-call(bf16[8,34,2176,128]{3,2,1,0:T(8,128)(2,1)} %get-tuple-element.10.slab), custom_call_target="tpu_custom_call" | custom-call | flops 10000000000 | bytes 142606336 | tf_op jit(solution)/shard_map/place_layers/pallas_call | solution.py:312
  966.9 59.5 %place_head.1 = bf16[37984,1024]{1,0:T(8,128)(2,1)} custom-call(bf16[8,34,2176,128]{3,2,1,0:T(8,128)(2,1)} %get-tuple-element.10.slab), custom_call_target="tpu_custom_call" | custom-call | flops 10000000000 | bytes 155582464 | tf_op jit(solution)/shard_map/place_head/pallas_call | solution.py:335
  1026.4 0.0 all-gather.3.cloned.1.call-done
  1026.4 12.2 %copy.14 = bf16[16,1024,256]{2,1,0:T(8,128)(2,1)} copy(bf16[16,1024,256]{1,2,0:T(8,128)(2,1)} %bitcast.3) | data formatting | bytes 16777216
  1038.6 48.6 %all-gather.5.cloned.1.call-done = bf16[16,704,1024]{2,1,0:T(8,128)(2,1)} async-done(((bf16[2,704,1024]{2,1,0:T(8,128)(2,1)}), bf16[16,704,1024]{2,1,0:T(8,128)(2,1)}) %all-gather.5.cloned.1.call-update) | async-done | bytes 23068688 | tf_op jit(solution)/shard_map/all_gather | solution.py:357
  1087.3 20.3 %copy.16 = bf16[16,1024,704]{1,2,0:T(8,128)(2,1)} copy(bf16[16,1024,704]{1,2,0:T(8,128)(2,1)} %bitcast.2) | data formatting | bytes 46137344
Async XLA Ops:
  7.2 1019.2 %all-gather.3.cloned.1.call-start = ((), (), s32[]{:S(2)}) async-start(), calls=%async_computation | async-start | bytes 9437184 | tf_op jit(solution)/shard_map/all_gather | solution.py:356
  912.8 174.5 %all-gather.5.cloned.1.call-start = ((), (), s32[]{:S(2)}) async-start(), calls=%async_computation.1 | async-start | bytes 25952256 | tf_op jit(solution)/shard_map/all_gather | solution.py:357
Sparse Core Ops, SparseCore 0:
  912.9 56.0 all-gather.2
  970.9 116.2 all-gather.4
